TPU v7x, 32 devices: a whole 2x2x4 slice. The times are simulated.
32 devices in a mesh: lat: 4 (over y, x), lon: 8 (over z, core).
Axes of the slice: x: 2, y: 2, z: 4, core: 2. Of those that a mesh axis runs over, the one named last changes fastest.
Arguments:
- transport: bfloat16 [48, 512, 3072], P(None, 'lat', 'lon'), may hold values from -0.0625 to 0.0625
- sigma_class: int32 [48, 512, 3072], P(None, 'lat', 'lon'), may hold values from 0 to 199
- basin_id: int32 [512, 3072], P('lat', 'lon'), may hold values from 0 to 3
- depth_levels: int32 [512, 3072], P('lat', 'lon'), may hold values from 0 to 48
Outputs:
- overturning: bfloat16 [4, 200, 512], replicated
Inputs may be any that keep to these rules, and one draw needn't show every extreme that they name: `depth_levels`: 0 marks a land column.
All inputs are finite; a program needn't handle non-finite values.
Results may differ from a plain program's by a relative error of at most 0.001.
Values may be sent and summed in bfloat16 or wider, within the bound.
A program may use at most 64 MiB of HBM per device.

v0:
```python
import jax
import jax.numpy as jnp
from jax import lax
from jax.sharding import PartitionSpec as P

CLASSES = 200
BASINS = 4


def bin_rows(transport, sigma_class, basin_id, depth_levels):
    depth_count, row_count, col_count = sigma_class.shape
    block_rows = 8
    block_count = row_count // block_rows
    cell_count = depth_count * col_count
    level_index = lax.broadcasted_iota(jnp.int32, (block_rows, depth_count, col_count), 1)
    class_iota = lax.broadcasted_iota(jnp.int32, (1, CLASSES, 1), 1)
    basin_iota = lax.broadcasted_iota(jnp.int32, (1, BASINS, 1), 1)

    def one_block(start):
        flow = jnp.transpose(lax.dynamic_slice_in_dim(transport, start, block_rows, 1), (1, 0, 2))
        klass = jnp.transpose(
            lax.dynamic_slice_in_dim(sigma_class, start, block_rows, 1), (1, 0, 2)
        )
        basin = lax.dynamic_slice_in_dim(basin_id, start, block_rows, 0)
        depth = lax.dynamic_slice_in_dim(depth_levels, start, block_rows, 0)
        wet_cells = level_index < depth[:, None, :]
        masked = jnp.where(wet_cells, flow, jnp.zeros_like(flow)).reshape(block_rows, 1, cell_count)
        basin_cells = jnp.broadcast_to(
            basin[:, None, :], (block_rows, depth_count, col_count)
        ).reshape(block_rows, 1, cell_count)
        basin_flow = jnp.where(basin_cells == basin_iota, masked, jnp.zeros_like(masked))
        class_hot = (klass.reshape(block_rows, 1, cell_count) == class_iota).astype(jnp.bfloat16)
        return jnp.einsum("rcn,rbn->rbc", class_hot, basin_flow, preferred_element_type=jnp.float32)

    starts = jnp.arange(block_count) * block_rows
    tables = lax.map(one_block, starts)
    return jnp.transpose(tables.reshape(row_count, BASINS, CLASSES), (1, 2, 0))


def body(transport, sigma_class, basin_id, depth_levels):
    table = bin_rows(transport, sigma_class, basin_id, depth_levels)
    shares = lax.psum_scatter(table, "lon", scatter_dimension=2, tiled=True)
    overturn = jnp.cumsum(shares, axis=1).astype(jnp.bfloat16)
    return lax.all_gather(overturn, ("lat", "lon"), axis=2, tiled=True)


def solution(mesh):
    placed = (P(None, "lat", "lon"), P(None, "lat", "lon"), P("lat", "lon"), P("lat", "lon"))
    return jax.shard_map(body, mesh=mesh, in_specs=placed, out_specs=P(), check_vma=False)
```

profile of v0, /device:TPU:0, one launch (start us, length us, event | category | flops | bytes accessed | tf_op | source)
XLA Modules:
  0.0 477.0 jit_solution(9716318747459529076)
XLA Ops:
  6.5 380.7 %while.11 = (s32[]{:T(128)}, f32[16,8,4,200]{3,2,1,0:T(4,128)S(1)}, s32[16]{0:T(128)S(1)}, s32[128,384]{1,0:T(8,128)}, s32[128,384]{1,0:T(8,128)}, /*index=5*/bf...) while((s32[]{:T(128)}, f32[16,8,4,200]{3,2,1,0:T(4,128)S(1)}, ...), condition=%wide.region_1.2_spmd.clone, body=%wide.region_0.1_spmd.clone.sunk | while | flops 266895360 | bytes 3940515 | solution.py:36
  9.3 0.8 constant_dynamic-slice_fusion.6
  10.1 1.2 fusion.29
  11.3 1.4 constant_dynamic-slice_fusion.5
  12.7 17.7 %fusion.30 = f32[16,8,4,200]{3,2,1,0:T(4,128)S(1)} fusion(f32[16,8,4,200]{3,2,1,0:T(4,128)S(1)} %get-tuple-element.150, s32[]{:T(128)} %get-tuple-element.149, s32[8,18432]{1,0:T(8,128)S(1)} %bitcast.46, s32[8,18432]{1,0:T(8,128)S(1)} %bitcast.45, bf16[8,18432]{1,0:T(8,128)(2,1)S(1)} %bitcast.47), kind=kOutput, calls=%fused_computation.10.clone.1 | convolution fusion | flops 266600448 | bytes 1507332 | tf_op jit(solution)/shard_map/while/body/eval_jaxpr/rcn,rbn->rbc/dot_general | solution.py:33
  33.1 0.8 constant_dynamic-slice_fusion.6
  33.9 1.2 fusion.29
  35.1 1.4 constant_dynamic-slice_fusion.5
  36.5 17.7 %fusion.30 = f32[16,8,4,200]{3,2,1,0:T(4,128)S(1)} fusion(f32[16,8,4,200]{3,2,1,0:T(4,128)S(1)} %get-tuple-element.150, s32[]{:T(128)} %get-tuple-element.149, s32[8,18432]{1,0:T(8,128)S(1)} %bitcast.46, s32[8,18432]{1,0:T(8,128)S(1)} %bitcast.45, bf16[8,18432]{1,0:T(8,128)(2,1)S(1)} %bitcast.47), kind=kOutput, calls=%fused_computation.10.clone.1 | convolution fusion | flops 266600448 | bytes 1507332 | tf_op jit(solution)/shard_map/while/body/eval_jaxpr/rcn,rbn->rbc/dot_general | solution.py:33
  56.9 0.8 constant_dynamic-slice_fusion.6
  57.7 1.2 fusion.29
  58.9 1.4 constant_dynamic-slice_fusion.5
  60.3 17.7 %fusion.30 = f32[16,8,4,200]{3,2,1,0:T(4,128)S(1)} fusion(f32[16,8,4,200]{3,2,1,0:T(4,128)S(1)} %get-tuple-element.150, s32[]{:T(128)} %get-tuple-element.149, s32[8,18432]{1,0:T(8,128)S(1)} %bitcast.46, s32[8,18432]{1,0:T(8,128)S(1)} %bitcast.45, bf16[8,18432]{1,0:T(8,128)(2,1)S(1)} %bitcast.47), kind=kOutput, calls=%fused_computation.10.clone.1 | convolution fusion | flops 266600448 | bytes 1507332 | tf_op jit(solution)/shard_map/while/body/eval_jaxpr/rcn,rbn->rbc/dot_general | solution.py:33
  80.7 0.8 constant_dynamic-slice_fusion.6
  81.5 1.2 fusion.29
  82.7 1.4 constant_dynamic-slice_fusion.5
  84.1 17.7 %fusion.30 = f32[16,8,4,200]{3,2,1,0:T(4,128)S(1)} fusion(f32[16,8,4,200]{3,2,1,0:T(4,128)S(1)} %get-tuple-element.150, s32[]{:T(128)} %get-tuple-element.149, s32[8,18432]{1,0:T(8,128)S(1)} %bitcast.46, s32[8,18432]{1,0:T(8,128)S(1)} %bitcast.45, bf16[8,18432]{1,0:T(8,128)(2,1)S(1)} %bitcast.47), kind=kOutput, calls=%fused_computation.10.clone.1 | convolution fusion | flops 266600448 | bytes 1507332 | tf_op jit(solution)/shard_map/while/body/eval_jaxpr/rcn,rbn->rbc/dot_general | solution.py:33
  104.5 0.8 constant_dynamic-slice_fusion.6
  105.3 1.2 fusion.29
  106.6 1.4 constant_dynamic-slice_fusion.5
  107.9 17.7 %fusion.30 = f32[16,8,4,200]{3,2,1,0:T(4,128)S(1)} fusion(f32[16,8,4,200]{3,2,1,0:T(4,128)S(1)} %get-tuple-element.150, s32[]{:T(128)} %get-tuple-element.149, s32[8,18432]{1,0:T(8,128)S(1)} %bitcast.46, s32[8,18432]{1,0:T(8,128)S(1)} %bitcast.45, bf16[8,18432]{1,0:T(8,128)(2,1)S(1)} %bitcast.47), kind=kOutput, calls=%fused_computation.10.clone.1 | convolution fusion | flops 266600448 | bytes 1507332 | tf_op jit(solution)/shard_map/while/body/eval_jaxpr/rcn,rbn->rbc/dot_general | solution.py:33
  128.4 0.8 constant_dynamic-slice_fusion.6
  129.1 1.2 fusion.29
  130.4 1.4 constant_dynamic-slice_fusion.5
  131.7 17.7 %fusion.30 = f32[16,8,4,200]{3,2,1,0:T(4,128)S(1)} fusion(f32[16,8,4,200]{3,2,1,0:T(4,128)S(1)} %get-tuple-element.150, s32[]{:T(128)} %get-tuple-element.149, s32[8,18432]{1,0:T(8,128)S(1)} %bitcast.46, s32[8,18432]{1,0:T(8,128)S(1)} %bitcast.45, bf16[8,18432]{1,0:T(8,128)(2,1)S(1)} %bitcast.47), kind=kOutput, calls=%fused_computation.10.clone.1 | convolution fusion | flops 266600448 | bytes 1507332 | tf_op jit(solution)/shard_map/while/body/eval_jaxpr/rcn,rbn->rbc/dot_general | solution.py:33
  152.2 0.8 constant_dynamic-slice_fusion.6
  152.9 1.2 fusion.29
  154.2 1.4 constant_dynamic-slice_fusion.5
  155.5 17.7 %fusion.30 = f32[16,8,4,200]{3,2,1,0:T(4,128)S(1)} fusion(f32[16,8,4,200]{3,2,1,0:T(4,128)S(1)} %get-tuple-element.150, s32[]{:T(128)} %get-tuple-element.149, s32[8,18432]{1,0:T(8,128)S(1)} %bitcast.46, s32[8,18432]{1,0:T(8,128)S(1)} %bitcast.45, bf16[8,18432]{1,0:T(8,128)(2,1)S(1)} %bitcast.47), kind=kOutput, calls=%fused_computation.10.clone.1 | convolution fusion | flops 266600448 | bytes 1507332 | tf_op jit(solution)/shard_map/while/body/eval_jaxpr/rcn,rbn->rbc/dot_general | solution.py:33
  176.0 0.8 constant_dynamic-slice_fusion.6
  176.8 1.2 fusion.29
  178.0 1.4 constant_dynamic-slice_fusion.5
  179.4 17.7 %fusion.30 = f32[16,8,4,200]{3,2,1,0:T(4,128)S(1)} fusion(f32[16,8,4,200]{3,2,1,0:T(4,128)S(1)} %get-tuple-element.150, s32[]{:T(128)} %get-tuple-element.149, s32[8,18432]{1,0:T(8,128)S(1)} %bitcast.46, s32[8,18432]{1,0:T(8,128)S(1)} %bitcast.45, bf16[8,18432]{1,0:T(8,128)(2,1)S(1)} %bitcast.47), kind=kOutput, calls=%fused_computation.10.clone.1 | convolution fusion | flops 266600448 | bytes 1507332 | tf_op jit(solution)/shard_map/while/body/eval_jaxpr/rcn,rbn->rbc/dot_general | solution.py:33
  199.8 0.8 constant_dynamic-slice_fusion.6
  200.6 1.2 fusion.29
  201.8 1.4 constant_dynamic-slice_fusion.5
  203.2 17.7 %fusion.30 = f32[16,8,4,200]{3,2,1,0:T(4,128)S(1)} fusion(f32[16,8,4,200]{3,2,1,0:T(4,128)S(1)} %get-tuple-element.150, s32[]{:T(128)} %get-tuple-element.149, s32[8,18432]{1,0:T(8,128)S(1)} %bitcast.46, s32[8,18432]{1,0:T(8,128)S(1)} %bitcast.45, bf16[8,18432]{1,0:T(8,128)(2,1)S(1)} %bitcast.47), kind=kOutput, calls=%fused_computation.10.clone.1 | convolution fusion | flops 266600448 | bytes 1507332 | tf_op jit(solution)/shard_map/while/body/eval_jaxpr/rcn,rbn->rbc/dot_general | solution.py:33
  224.4 1.2 fusion.29
  225.6 1.4 constant_dynamic-slice_fusion.5
  227.0 17.7 %fusion.30 = f32[16,8,4,200]{3,2,1,0:T(4,128)S(1)} fusion(f32[16,8,4,200]{3,2,1,0:T(4,128)S(1)} %get-tuple-element.150, s32[]{:T(128)} %get-tuple-element.149, s32[8,18432]{1,0:T(8,128)S(1)} %bitcast.46, s32[8,18432]{1,0:T(8,128)S(1)} %bitcast.45, bf16[8,18432]{1,0:T(8,128)(2,1)S(1)} %bitcast.47), kind=kOutput, calls=%fused_computation.10.clone.1 | convolution fusion | flops 266600448 | bytes 1507332 | tf_op jit(solution)/shard_map/while/body/eval_jaxpr/rcn,rbn->rbc/dot_general | solution.py:33
  248.2 1.2 fusion.29
  249.4 1.4 constant_dynamic-slice_fusion.5
  250.8 17.7 %fusion.30 = f32[16,8,4,200]{3,2,1,0:T(4,128)S(1)} fusion(f32[16,8,4,200]{3,2,1,0:T(4,128)S(1)} %get-tuple-element.150, s32[]{:T(128)} %get-tuple-element.149, s32[8,18432]{1,0:T(8,128)S(1)} %bitcast.46, s32[8,18432]{1,0:T(8,128)S(1)} %bitcast.45, bf16[8,18432]{1,0:T(8,128)(2,1)S(1)} %bitcast.47), kind=kOutput, calls=%fused_computation.10.clone.1 | convolution fusion | flops 266600448 | bytes 1507332 | tf_op jit(solution)/shard_map/while/body/eval_jaxpr/rcn,rbn->rbc/dot_general | solution.py:33
  272.0 1.2 fusion.29
  273.3 1.4 constant_dynamic-slice_fusion.5
  274.6 17.7 %fusion.30 = f32[16,8,4,200]{3,2,1,0:T(4,128)S(1)} fusion(f32[16,8,4,200]{3,2,1,0:T(4,128)S(1)} %get-tuple-element.150, s32[]{:T(128)} %get-tuple-element.149, s32[8,18432]{1,0:T(8,128)S(1)} %bitcast.46, s32[8,18432]{1,0:T(8,128)S(1)} %bitcast.45, bf16[8,18432]{1,0:T(8,128)(2,1)S(1)} %bitcast.47), kind=kOutput, calls=%fused_computation.10.clone.1 | convolution fusion | flops 266600448 | bytes 1507332 | tf_op jit(solution)/shard_map/while/body/eval_jaxpr/rcn,rbn->rbc/dot_general | solution.py:33
  295.8 1.2 fusion.29
  297.1 1.4 constant_dynamic-slice_fusion.5
  298.4 17.7 %fusion.30 = f32[16,8,4,200]{3,2,1,0:T(4,128)S(1)} fusion(f32[16,8,4,200]{3,2,1,0:T(4,128)S(1)} %get-tuple-element.150, s32[]{:T(128)} %get-tuple-element.149, s32[8,18432]{1,0:T(8,128)S(1)} %bitcast.46, s32[8,18432]{1,0:T(8,128)S(1)} %bitcast.45, bf16[8,18432]{1,0:T(8,128)(2,1)S(1)} %bitcast.47), kind=kOutput, calls=%fused_computation.10.clone.1 | convolution fusion | flops 266600448 | bytes 1507332 | tf_op jit(solution)/shard_map/while/body/eval_jaxpr/rcn,rbn->rbc/dot_general | solution.py:33
  319.6 1.2 fusion.29
  320.9 1.4 constant_dynamic-slice_fusion.5
  322.2 17.7 %fusion.30 = f32[16,8,4,200]{3,2,1,0:T(4,128)S(1)} fusion(f32[16,8,4,200]{3,2,1,0:T(4,128)S(1)} %get-tuple-element.150, s32[]{:T(128)} %get-tuple-element.149, s32[8,18432]{1,0:T(8,128)S(1)} %bitcast.46, s32[8,18432]{1,0:T(8,128)S(1)} %bitcast.45, bf16[8,18432]{1,0:T(8,128)(2,1)S(1)} %bitcast.47), kind=kOutput, calls=%fused_computation.10.clone.1 | convolution fusion | flops 266600448 | bytes 1507332 | tf_op jit(solution)/shard_map/while/body/eval_jaxpr/rcn,rbn->rbc/dot_general | solution.py:33
  343.5 1.2 fusion.29
  344.7 1.4 constant_dynamic-slice_fusion.5
  346.1 17.7 %fusion.30 = f32[16,8,4,200]{3,2,1,0:T(4,128)S(1)} fusion(f32[16,8,4,200]{3,2,1,0:T(4,128)S(1)} %get-tuple-element.150, s32[]{:T(128)} %get-tuple-element.149, s32[8,18432]{1,0:T(8,128)S(1)} %bitcast.46, s32[8,18432]{1,0:T(8,128)S(1)} %bitcast.45, bf16[8,18432]{1,0:T(8,128)(2,1)S(1)} %bitcast.47), kind=kOutput, calls=%fused_computation.10.clone.1 | convolution fusion | flops 266600448 | bytes 1507332 | tf_op jit(solution)/shard_map/while/body/eval_jaxpr/rcn,rbn->rbc/dot_general | solution.py:33
  367.2 1.1 fusion.29
  368.4 1.1 constant_dynamic-slice_fusion.5
  369.5 17.7 %fusion.30 = f32[16,8,4,200]{3,2,1,0:T(4,128)S(1)} fusion(f32[16,8,4,200]{3,2,1,0:T(4,128)S(1)} %get-tuple-element.150, s32[]{:T(128)} %get-tuple-element.149, s32[8,18432]{1,0:T(8,128)S(1)} %bitcast.46, s32[8,18432]{1,0:T(8,128)S(1)} %bitcast.45, bf16[8,18432]{1,0:T(8,128)(2,1)S(1)} %bitcast.47), kind=kOutput, calls=%fused_computation.10.clone.1 | convolution fusion | flops 266600448 | bytes 1507332 | tf_op jit(solution)/shard_map/while/body/eval_jaxpr/rcn,rbn->rbc/dot_general | solution.py:33
  387.2 0.9 copy.18
  388.1 34.0 %reduce-scatter.2.cloned.1.call-done = f32[4,200,16]{1,2,0:T(8,128)} async-done(((f32[4,200,128]{1,2,0:T(8,128)}), f32[4,200,16]{1,2,0:T(8,128)}) %reduce-scatter.2.cloned.1.call-update) | async-done | bytes 51216 | tf_op jit(solution)/shard_map/reduce_scatter | solution.py:42
  422.2 0.8 copy_bitcast_fusion.1
  423.0 2.3 reduce-window.6
  425.6 43.3 %all_gather.3 = bf16[4,200,512]{1,2,0:T(8,128)(2,1)S(1)} all-gather(bf16[4,200,16]{1,2,0:T(8,128)(2,1)S(1)} %bitcast.50), channel_id=1, replica_groups=mesh['lat'=4,'lon'=8] {'lat','lon'}, dimensions={2}, use_global_device_ids=true | all-gather | bytes 844800 | tf_op jit(solution)/shard_map/all_gather | solution.py:44
  468.9 1.2 copy.12
  (49 shorter events, 17.0 us)
Async XLA Ops:
  6.5 415.6 %reduce-scatter.2.cloned.1.call-start = ((), (), s32[]{:S(2)}) async-start(), calls=%async_computation.1 | async-start | bytes 589824 | tf_op jit(solution)/shard_map/reduce_scatter | solution.py:42
Sparse Core Ops, SparseCore 0:
  388.3 33.8 reduce-scatter.1
where the time goes:
time: 480 us; the launch traced here: 477 us
  matrix products  283 us (59%)
  local copies, waits for them, and re-layouts  48.3 us (10%)
  blocking collectives  43.3 us (9%)
  waiting for transfers between devices  34 us (7%)
  loops' own time  33.4 us (7%)
  other arithmetic  21.5 us (4%)
  between operations  13.4 us (3%)
    dot_general x16, matrix products, one_block(): jnp.einsum('rcn,rbn->rbc', class_hot, basin_flow, preferred_element_type=...  283 us
    all_gather x1, blocking collectives, body(): return lax.all_gather(overturn, ('lat', 'lon'), axis=2, tiled=True)  43.3 us
    reduce_scatter x1, waiting for transfers between devices, body(): shares = lax.psum_scatter(table, 'lon', scatter_dimension=2, tiled=True)  34 us
    another operation x1, loops' own time, bin_rows(): tables = lax.map(one_block, starts)  33.4 us
    dynamic_slice x16, local copies, waits for them, and re-layouts, one_block(): lax.dynamic_slice_in_dim(sigma_class, start, block_rows, 1)  21.4 us
    select_n x16, other arithmetic, one_block(): jnp.where(wet_cells, flow, jnp.zeros_like(flow))  19.1 us
    dynamic_slice x16, local copies, waits for them, and re-layouts, one_block(): depth = lax.dynamic_slice_in_dim(depth_levels, start, block_rows, 0)  12.3 us
    dynamic_slice x16, local copies, waits for them, and re-layouts, bin_rows(): tables = lax.map(one_block, starts)  10.7 us
  transfers between devices with their start and end apart: 1, of which 1 were waited for; matrix products, arithmetic and copies ran while one was open for 0% of the time, Pallas kernels for 0%

commit v1 on v0

--- a/solution.py
+++ b/solution.py
@@ -1,3 +1,4 @@
+import functools
 import jax
 import jax.numpy as jnp
 from jax import lax
@@ -5,6 +6,13 @@
 
 CLASSES = 200
 BASINS = 4
+
+
+def launch_marks(message, axis_id):
+    return jnp.concatenate(lax.all_gather(message, axis_id), axis=2)
+
+
+wait_ranges = functools.partial(launch_marks, axis_id=("lat", "lon"))
 
 
 def bin_rows(transport, sigma_class, basin_id, depth_levels):
@@ -41,7 +49,7 @@
     table = bin_rows(transport, sigma_class, basin_id, depth_levels)
     shares = lax.psum_scatter(table, "lon", scatter_dimension=2, tiled=True)
     overturn = jnp.cumsum(shares, axis=1).astype(jnp.bfloat16)
-    return lax.all_gather(overturn, ("lat", "lon"), axis=2, tiled=True)
+    return wait_ranges(overturn)
 
 
 def solution(mesh):

time: 480 us -> 480 us (level)
  no operation moved by 1% of the time
where the time goes in v1:
time: 480 us; the launch traced here: 477 us
  matrix products  283 us (59%)
  local copies, waits for them, and re-layouts  48.3 us (10%)
  blocking collectives  43.3 us (9%)
  waiting for transfers between devices  34 us (7%)
  loops' own time  33.4 us (7%)
  other arithmetic  21.5 us (4%)
  between operations  13.4 us (3%)
    dot_general x16, matrix products, one_block(): jnp.einsum('rcn,rbn->rbc', class_hot, basin_flow, preferred_element_type=...  283 us
    all_gather x1, blocking collectives, launch_marks(): return jnp.concatenate(lax.all_gather(message, axis_id), axis=2)  43.3 us
    reduce_scatter x1, waiting for transfers between devices, body(): shares = lax.psum_scatter(table, 'lon', scatter_dimension=2, tiled=True)  34 us
    another operation x1, loops' own time, bin_rows(): tables = lax.map(one_block, starts)  33.4 us
    dynamic_slice x16, local copies, waits for them, and re-layouts, one_block(): lax.dynamic_slice_in_dim(sigma_class, start, block_rows, 1)  21.4 us
    select_n x16, other arithmetic, one_block(): jnp.where(wet_cells, flow, jnp.zeros_like(flow))  19.1 us
    dynamic_slice x16, local copies, waits for them, and re-layouts, one_block(): depth = lax.dynamic_slice_in_dim(depth_levels, start, block_rows, 0)  12.3 us
    dynamic_slice x16, local copies, waits for them, and re-layouts, bin_rows(): tables = lax.map(one_block, starts)  10.7 us
  transfers between devices with their start and end apart: 1, of which 1 were waited for; matrix products, arithmetic and copies ran while one was open for 0% of the time, Pallas kernels for 0%

profile of v1, /device:TPU:0, one launch (start us, length us, event | category | flops | bytes accessed | tf_op | source)
XLA Modules:
  0.0 477.1 jit_solution(13743657388425474255)
XLA Ops:
  6.5 380.7 %while.11 = (s32[]{:T(128)}, f32[16,8,4,200]{3,2,1,0:T(4,128)S(1)}, s32[16]{0:T(128)S(1)}, s32[128,384]{1,0:T(8,128)}, s32[128,384]{1,0:T(8,128)}, /*index=5*/bf...) while((s32[]{:T(128)}, f32[16,8,4,200]{3,2,1,0:T(4,128)S(1)}, ...), condition=%wide.region_1.2_spmd.clone, body=%wide.region_0.1_spmd.clone.sunk | while | flops 266895360 | bytes 3940515 | solution.py:44
  9.3 0.8 constant_dynamic-slice_fusion.6
  10.1 1.2 fusion.29
  11.3 1.4 constant_dynamic-slice_fusion.5
  12.7 17.7 %fusion.30 = f32[16,8,4,200]{3,2,1,0:T(4,128)S(1)} fusion(f32[16,8,4,200]{3,2,1,0:T(4,128)S(1)} %get-tuple-element.150, s32[]{:T(128)} %get-tuple-element.149, s32[8,18432]{1,0:T(8,128)S(1)} %bitcast.50, s32[8,18432]{1,0:T(8,128)S(1)} %bitcast.49, bf16[8,18432]{1,0:T(8,128)(2,1)S(1)} %bitcast.51), kind=kOutput, calls=%fused_computation.10.clone.1 | convolution fusion | flops 266600448 | bytes 1507332 | tf_op jit(solution)/shard_map/while/body/eval_jaxpr/rcn,rbn->rbc/dot_general | solution.py:41
  33.1 0.8 constant_dynamic-slice_fusion.6
  33.9 1.2 fusion.29
  35.1 1.4 constant_dynamic-slice_fusion.5
  36.5 17.7 %fusion.30 = f32[16,8,4,200]{3,2,1,0:T(4,128)S(1)} fusion(f32[16,8,4,200]{3,2,1,0:T(4,128)S(1)} %get-tuple-element.150, s32[]{:T(128)} %get-tuple-element.149, s32[8,18432]{1,0:T(8,128)S(1)} %bitcast.50, s32[8,18432]{1,0:T(8,128)S(1)} %bitcast.49, bf16[8,18432]{1,0:T(8,128)(2,1)S(1)} %bitcast.51), kind=kOutput, calls=%fused_computation.10.clone.1 | convolution fusion | flops 266600448 | bytes 1507332 | tf_op jit(solution)/shard_map/while/body/eval_jaxpr/rcn,rbn->rbc/dot_general | solution.py:41
  56.9 0.8 constant_dynamic-slice_fusion.6
  57.7 1.2 fusion.29
  58.9 1.4 constant_dynamic-slice_fusion.5
  60.3 17.7 %fusion.30 = f32[16,8,4,200]{3,2,1,0:T(4,128)S(1)} fusion(f32[16,8,4,200]{3,2,1,0:T(4,128)S(1)} %get-tuple-element.150, s32[]{:T(128)} %get-tuple-element.149, s32[8,18432]{1,0:T(8,128)S(1)} %bitcast.50, s32[8,18432]{1,0:T(8,128)S(1)} %bitcast.49, bf16[8,18432]{1,0:T(8,128)(2,1)S(1)} %bitcast.51), kind=kOutput, calls=%fused_computation.10.clone.1 | convolution fusion | flops 266600448 | bytes 1507332 | tf_op jit(solution)/shard_map/while/body/eval_jaxpr/rcn,rbn->rbc/dot_general | solution.py:41
  80.7 0.8 constant_dynamic-slice_fusion.6
  81.5 1.2 fusion.29
  82.7 1.4 constant_dynamic-slice_fusion.5
  84.1 17.7 %fusion.30 = f32[16,8,4,200]{3,2,1,0:T(4,128)S(1)} fusion(f32[16,8,4,200]{3,2,1,0:T(4,128)S(1)} %get-tuple-element.150, s32[]{:T(128)} %get-tuple-element.149, s32[8,18432]{1,0:T(8,128)S(1)} %bitcast.50, s32[8,18432]{1,0:T(8,128)S(1)} %bitcast.49, bf16[8,18432]{1,0:T(8,128)(2,1)S(1)} %bitcast.51), kind=kOutput, calls=%fused_computation.10.clone.1 | convolution fusion | flops 266600448 | bytes 1507332 | tf_op jit(solution)/shard_map/while/body/eval_jaxpr/rcn,rbn->rbc/dot_general | solution.py:41
  104.5 0.8 constant_dynamic-slice_fusion.6
  105.3 1.2 fusion.29
  106.6 1.4 constant_dynamic-slice_fusion.5
  107.9 17.7 %fusion.30 = f32[16,8,4,200]{3,2,1,0:T(4,128)S(1)} fusion(f32[16,8,4,200]{3,2,1,0:T(4,128)S(1)} %get-tuple-element.150, s32[]{:T(128)} %get-tuple-element.149, s32[8,18432]{1,0:T(8,128)S(1)} %bitcast.50, s32[8,18432]{1,0:T(8,128)S(1)} %bitcast.49, bf16[8,18432]{1,0:T(8,128)(2,1)S(1)} %bitcast.51), kind=kOutput, calls=%fused_computation.10.clone.1 | convolution fusion | flops 266600448 | bytes 1507332 | tf_op jit(solution)/shard_map/while/body/eval_jaxpr/rcn,rbn->rbc/dot_general | solution.py:41
  128.4 0.8 constant_dynamic-slice_fusion.6
  129.1 1.2 fusion.29
  130.4 1.4 constant_dynamic-slice_fusion.5
  131.7 17.7 %fusion.30 = f32[16,8,4,200]{3,2,1,0:T(4,128)S(1)} fusion(f32[16,8,4,200]{3,2,1,0:T(4,128)S(1)} %get-tuple-element.150, s32[]{:T(128)} %get-tuple-element.149, s32[8,18432]{1,0:T(8,128)S(1)} %bitcast.50, s32[8,18432]{1,0:T(8,128)S(1)} %bitcast.49, bf16[8,18432]{1,0:T(8,128)(2,1)S(1)} %bitcast.51), kind=kOutput, calls=%fused_computation.10.clone.1 | convolution fusion | flops 266600448 | bytes 1507332 | tf_op jit(solution)/shard_map/while/body/eval_jaxpr/rcn,rbn->rbc/dot_general | solution.py:41
  152.2 0.8 constant_dynamic-slice_fusion.6
  152.9 1.2 fusion.29
  154.2 1.4 constant_dynamic-slice_fusion.5
  155.5 17.7 %fusion.30 = f32[16,8,4,200]{3,2,1,0:T(4,128)S(1)} fusion(f32[16,8,4,200]{3,2,1,0:T(4,128)S(1)} %get-tuple-element.150, s32[]{:T(128)} %get-tuple-element.149, s32[8,18432]{1,0:T(8,128)S(1)} %bitcast.50, s32[8,18432]{1,0:T(8,128)S(1)} %bitcast.49, bf16[8,18432]{1,0:T(8,128)(2,1)S(1)} %bitcast.51), kind=kOutput, calls=%fused_computation.10.clone.1 | convolution fusion | flops 266600448 | bytes 1507332 | tf_op jit(solution)/shard_map/while/body/eval_jaxpr/rcn,rbn->rbc/dot_general | solution.py:41
  176.0 0.8 constant_dynamic-slice_fusion.6
  176.8 1.2 fusion.29
  178.0 1.4 constant_dynamic-slice_fusion.5
  179.4 17.7 %fusion.30 = f32[16,8,4,200]{3,2,1,0:T(4,128)S(1)} fusion(f32[16,8,4,200]{3,2,1,0:T(4,128)S(1)} %get-tuple-element.150, s32[]{:T(128)} %get-tuple-element.149, s32[8,18432]{1,0:T(8,128)S(1)} %bitcast.50, s32[8,18432]{1,0:T(8,128)S(1)} %bitcast.49, bf16[8,18432]{1,0:T(8,128)(2,1)S(1)} %bitcast.51), kind=kOutput, calls=%fused_computation.10.clone.1 | convolution fusion | flops 266600448 | bytes 1507332 | tf_op jit(solution)/shard_map/while/body/eval_jaxpr/rcn,rbn->rbc/dot_general | solution.py:41
  199.8 0.8 constant_dynamic-slice_fusion.6
  200.6 1.2 fusion.29
  201.8 1.4 constant_dynamic-slice_fusion.5
  203.2 17.7 %fusion.30 = f32[16,8,4,200]{3,2,1,0:T(4,128)S(1)} fusion(f32[16,8,4,200]{3,2,1,0:T(4,128)S(1)} %get-tuple-element.150, s32[]{:T(128)} %get-tuple-element.149, s32[8,18432]{1,0:T(8,128)S(1)} %bitcast.50, s32[8,18432]{1,0:T(8,128)S(1)} %bitcast.49, bf16[8,18432]{1,0:T(8,128)(2,1)S(1)} %bitcast.51), kind=kOutput, calls=%fused_computation.10.clone.1 | convolution fusion | flops 266600448 | bytes 1507332 | tf_op jit(solution)/shard_map/while/body/eval_jaxpr/rcn,rbn->rbc/dot_general | solution.py:41
  224.4 1.2 fusion.29
  225.6 1.4 constant_dynamic-slice_fusion.5
  227.0 17.7 %fusion.30 = f32[16,8,4,200]{3,2,1,0:T(4,128)S(1)} fusion(f32[16,8,4,200]{3,2,1,0:T(4,128)S(1)} %get-tuple-element.150, s32[]{:T(128)} %get-tuple-element.149, s32[8,18432]{1,0:T(8,128)S(1)} %bitcast.50, s32[8,18432]{1,0:T(8,128)S(1)} %bitcast.49, bf16[8,18432]{1,0:T(8,128)(2,1)S(1)} %bitcast.51), kind=kOutput, calls=%fused_computation.10.clone.1 | convolution fusion | flops 266600448 | bytes 1507332 | tf_op jit(solution)/shard_map/while/body/eval_jaxpr/rcn,rbn->rbc/dot_general | solution.py:41
  248.2 1.2 fusion.29
  249.4 1.4 constant_dynamic-slice_fusion.5
  250.8 17.7 %fusion.30 = f32[16,8,4,200]{3,2,1,0:T(4,128)S(1)} fusion(f32[16,8,4,200]{3,2,1,0:T(4,128)S(1)} %get-tuple-element.150, s32[]{:T(128)} %get-tuple-element.149, s32[8,18432]{1,0:T(8,128)S(1)} %bitcast.50, s32[8,18432]{1,0:T(8,128)S(1)} %bitcast.49, bf16[8,18432]{1,0:T(8,128)(2,1)S(1)} %bitcast.51), kind=kOutput, calls=%fused_computation.10.clone.1 | convolution fusion | flops 266600448 | bytes 1507332 | tf_op jit(solution)/shard_map/while/body/eval_jaxpr/rcn,rbn->rbc/dot_general | solution.py:41
  272.0 1.2 fusion.29
  273.3 1.4 constant_dynamic-slice_fusion.5
  274.6 17.7 %fusion.30 = f32[16,8,4,200]{3,2,1,0:T(4,128)S(1)} fusion(f32[16,8,4,200]{3,2,1,0:T(4,128)S(1)} %get-tuple-element.150, s32[]{:T(128)} %get-tuple-element.149, s32[8,18432]{1,0:T(8,128)S(1)} %bitcast.50, s32[8,18432]{1,0:T(8,128)S(1)} %bitcast.49, bf16[8,18432]{1,0:T(8,128)(2,1)S(1)} %bitcast.51), kind=kOutput, calls=%fused_computation.10.clone.1 | convolution fusion | flops 266600448 | bytes 1507332 | tf_op jit(solution)/shard_map/while/body/eval_jaxpr/rcn,rbn->rbc/dot_general | solution.py:41
  295.8 1.2 fusion.29
  297.1 1.4 constant_dynamic-slice_fusion.5
  298.4 17.7 %fusion.30 = f32[16,8,4,200]{3,2,1,0:T(4,128)S(1)} fusion(f32[16,8,4,200]{3,2,1,0:T(4,128)S(1)} %get-tuple-element.150, s32[]{:T(128)} %get-tuple-element.149, s32[8,18432]{1,0:T(8,128)S(1)} %bitcast.50, s32[8,18432]{1,0:T(8,128)S(1)} %bitcast.49, bf16[8,18432]{1,0:T(8,128)(2,1)S(1)} %bitcast.51), kind=kOutput, calls=%fused_computation.10.clone.1 | convolution fusion | flops 266600448 | bytes 1507332 | tf_op jit(solution)/shard_map/while/body/eval_jaxpr/rcn,rbn->rbc/dot_general | solution.py:41
  319.6 1.2 fusion.29
  320.9 1.4 constant_dynamic-slice_fusion.5
  322.2 17.7 %fusion.30 = f32[16,8,4,200]{3,2,1,0:T(4,128)S(1)} fusion(f32[16,8,4,200]{3,2,1,0:T(4,128)S(1)} %get-tuple-element.150, s32[]{:T(128)} %get-tuple-element.149, s32[8,18432]{1,0:T(8,128)S(1)} %bitcast.50, s32[8,18432]{1,0:T(8,128)S(1)} %bitcast.49, bf16[8,18432]{1,0:T(8,128)(2,1)S(1)} %bitcast.51), kind=kOutput, calls=%fused_computation.10.clone.1 | convolution fusion | flops 266600448 | bytes 1507332 | tf_op jit(solution)/shard_map/while/body/eval_jaxpr/rcn,rbn->rbc/dot_general | solution.py:41
  343.5 1.2 fusion.29
  344.7 1.4 constant_dynamic-slice_fusion.5
  346.1 17.7 %fusion.30 = f32[16,8,4,200]{3,2,1,0:T(4,128)S(1)} fusion(f32[16,8,4,200]{3,2,1,0:T(4,128)S(1)} %get-tuple-element.150, s32[]{:T(128)} %get-tuple-element.149, s32[8,18432]{1,0:T(8,128)S(1)} %bitcast.50, s32[8,18432]{1,0:T(8,128)S(1)} %bitcast.49, bf16[8,18432]{1,0:T(8,128)(2,1)S(1)} %bitcast.51), kind=kOutput, calls=%fused_computation.10.clone.1 | convolution fusion | flops 266600448 | bytes 1507332 | tf_op jit(solution)/shard_map/while/body/eval_jaxpr/rcn,rbn->rbc/dot_general | solution.py:41
  367.2 1.1 fusion.29
  368.4 1.1 constant_dynamic-slice_fusion.5
  369.5 17.7 %fusion.30 = f32[16,8,4,200]{3,2,1,0:T(4,128)S(1)} fusion(f32[16,8,4,200]{3,2,1,0:T(4,128)S(1)} %get-tuple-element.150, s32[]{:T(128)} %get-tuple-element.149, s32[8,18432]{1,0:T(8,128)S(1)} %bitcast.50, s32[8,18432]{1,0:T(8,128)S(1)} %bitcast.49, bf16[8,18432]{1,0:T(8,128)(2,1)S(1)} %bitcast.51), kind=kOutput, calls=%fused_computation.10.clone.1 | convolution fusion | flops 266600448 | bytes 1507332 | tf_op jit(solution)/shard_map/while/body/eval_jaxpr/rcn,rbn->rbc/dot_general | solution.py:41
  387.2 0.9 copy.26
  388.1 34.0 %reduce-scatter.2.cloned.1.call-done = f32[4,200,16]{1,2,0:T(8,128)} async-done(((f32[4,200,128]{1,2,0:T(8,128)}), f32[4,200,16]{1,2,0:T(8,128)}) %reduce-scatter.2.cloned.1.call-update) | async-done | bytes 51216 | tf_op jit(solution)/shard_map/reduce_scatter | solution.py:50
  422.2 0.8 copy_bitcast_fusion.1
  423.0 2.3 reduce-window.6
  425.6 43.3 %all-gather = bf16[128,200,16]{1,2,0:T(8,128)(2,1)S(1)} all-gather(bf16[4,200,16]{1,2,0:T(8,128)(2,1)S(1)} %bitcast.56), channel_id=2, replica_groups=mesh['lat'=4,'lon'=8] {'lat','lon'}, dimensions={0}, use_global_device_ids=true | all-gather | bytes 844800 | tf_op jit(solution)/shard_map/all_gather | solution.py:12
  469.0 1.3 copy.20
  (50 shorter events, 17.1 us)
Async XLA Ops:
  6.5 415.6 %reduce-scatter.2.cloned.1.call-start = ((), (), s32[]{:S(2)}) async-start(), calls=%async_computation.1 | async-start | bytes 589824 | tf_op jit(solution)/shard_map/reduce_scatter | solution.py:50
Sparse Core Ops, SparseCore 0:
  388.3 33.8 reduce-scatter.1
